TPU v7x, 256 devices: a whole 4x4x8 slice. The times are simulated.
256 devices in a mesh: fsdp: 32 (over y, x, z_lo), rep: 8 (over z_hi, core).
Axes of the slice: x: 4, y: 4, z: 8 (z_hi: 4, z_lo: 2; z = z_hi * 2 + z_lo), core: 2. Of those that a mesh axis runs over, the one named last changes fastest.
Arguments:
- tokens: bfloat16 [122880, 3584], P(('fsdp', 'rep')), may hold values from -6 to 6
- positions: int32 [122880], P(('fsdp', 'rep')), may hold values from 0 to 4095
- slow_weight: float32 [3584, 4096], P('fsdp', 'rep'), may hold values from -0.09375 to 0.09375
- fast_weight: bfloat16 [8, 3584, 4096], P('rep', 'fsdp'), may hold values from -0.125 to 0.125
- slow_gain: float32 [3584], P(('fsdp', 'rep')), may hold values from -3 to 3
- fast_gain: bfloat16 [8, 3584], P('rep', 'fsdp'), may hold values from -3 to 3
Outputs:
- query_states: bfloat16 [122880, 2048], P(('fsdp', 'rep'))
- key_states: bfloat16 [122880, 1024], P(('fsdp', 'rep'))
- value_states: bfloat16 [122880, 1024], P(('fsdp', 'rep'))
- new_weight: float32 [3584, 4096], P('fsdp', 'rep')
- new_gain: float32 [3584], P(('fsdp', 'rep'))
All inputs are finite; a program needn't handle non-finite values.
Results may differ from a plain program's by a relative error of at most 0.012.
Values may be sent and summed in bfloat16 or wider, within the bound.
A program may use at most 128 MiB of HBM per device.

v0:
```python
import jax
import jax.numpy as jnp
from jax import lax
from jax.sharding import PartitionSpec as P

QHEADS = 8
KVHEADS = 4
HEAD = 256


EPSILON = 1e-06
ADVANCE_RATE = 0.5
ROPE_BASE = 10000.0


def cut_along(x, dim, devices):
    lengths = x.shape
    tiles = x.reshape(*lengths[:dim], devices, lengths[dim] // devices, *lengths[dim + 1 :])
    return jnp.moveaxis(tiles, dim, 0)


def one_scatter(arrays, axis, dims):
    devices = lax.axis_size(axis)
    tiles = [cut_along(a, dim, devices) for a, dim in zip(arrays, dims)]
    lines = jnp.concatenate([b.reshape(devices, -1) for b in tiles], axis=1)
    width = max(16, -(-lines.shape[1] // 1024) * 8)
    lines = jnp.pad(lines, ((0, 0), (0, width * 128 - lines.shape[1]))).reshape(-1, 128)
    line, at, done = (lax.psum_scatter(lines, axis, tiled=True).reshape(-1), 0, [])
    for b in tiles:
        part = b[0]
        done.append(line[at : at + part.size].reshape(part.shape))
        at += part.size
    return tuple(done)


def rotate(values, positions, head_count):
    row_count = values.shape[0]
    head_width = values.shape[1] // head_count
    half_width = head_width // 2
    by_head = values.reshape(row_count, head_count, head_width)
    inverse_rates = ROPE_BASE ** (-(jnp.arange(half_width, dtype=jnp.float32) * 2.0 / head_width))
    angles = positions.astype(jnp.float32)[:, None] * inverse_rates[None, :]
    cosine_table = jnp.cos(angles)[:, None, :]
    sine_table = jnp.sin(angles)[:, None, :]
    front_half = by_head[:, :, :half_width]
    back_half = by_head[:, :, half_width:]
    turned = jnp.concatenate(
        [
            front_half * cosine_table - back_half * sine_table,
            back_half * cosine_table + front_half * sine_table,
        ],
        axis=2,
    )
    return turned.reshape(row_count, head_count * head_width)


def on_device(tokens, positions, slow_weight, fast_weight, slow_gain, fast_gain):
    replicas = lax.axis_size("rep")
    totals = tuple(
        (
            part.astype(jnp.float32)
            for part in one_scatter(
                (
                    fast_weight.astype(jnp.float32).astype(jnp.bfloat16),
                    fast_gain.astype(jnp.float32).astype(jnp.bfloat16),
                ),
                "rep",
                (2, 1),
            )
        )
    )
    new_weight = slow_weight + ADVANCE_RATE * (totals[0][0] / replicas - slow_weight)
    new_gain = slow_gain + ADVANCE_RATE * (totals[1][0] / replicas - slow_gain)
    own_weight = new_weight.astype(jnp.bfloat16)
    own_gain = new_gain.astype(jnp.bfloat16)
    floats = tokens.astype(jnp.float32)
    inv_rms = lax.rsqrt(jnp.mean(floats * floats, axis=1, keepdims=True) + EPSILON)
    column_weight = lax.all_gather(own_weight, "fsdp", axis=0, tiled=True)
    whole_gain = lax.all_gather(own_gain, ("fsdp", "rep"), axis=0, tiled=True)
    normed = (floats * inv_rms * (1.0 + whole_gain.astype(jnp.float32))[None, :]).astype(
        jnp.bfloat16
    )
    projected = jnp.dot(
        normed,
        lax.all_gather(column_weight, "rep", axis=1, tiled=True),
        preferred_element_type=jnp.float32,
    )
    query_cols = QHEADS * HEAD
    key_cols = KVHEADS * HEAD
    query_states = rotate(projected[:, :query_cols], positions, QHEADS).astype(jnp.bfloat16)
    key_states = rotate(
        projected[:, query_cols : query_cols + key_cols], positions, KVHEADS
    ).astype(jnp.bfloat16)
    value_states = projected[:, query_cols + key_cols :].astype(jnp.bfloat16)
    return (query_states, key_states, value_states, new_weight, new_gain)


def solution(mesh):
    return jax.shard_map(
        on_device,
        mesh=mesh,
        in_specs=(
            P(("fsdp", "rep"), None),
            P(("fsdp", "rep")),
            P("fsdp", "rep"),
            P("rep", "fsdp", None),
            P(("fsdp", "rep")),
            P("rep", "fsdp"),
        ),
        out_specs=(
            P(("fsdp", "rep"), None),
            P(("fsdp", "rep"), None),
            P(("fsdp", "rep"), None),
            P("fsdp", "rep"),
            P(("fsdp", "rep")),
        ),
        check_vma=False,
    )
```

profile of v0, /device:TPU:35, one launch (start us, length us, event | category | flops | bytes accessed | tf_op | source)
XLA Modules:
  0.0 565.5 jit_solution(11715870747473245055)
XLA Ops:
  7.2 0.0 copy-start.5
  7.2 0.0 all-reduce.5.cloned.1.call-start
  7.2 1.5 copy.11
  8.7 0.5 broadcast.84
  9.2 1.3 reduce.3
  10.6 0.1 reshape_transpose_reshape.3
  10.7 0.1 fusion.9
  10.7 1.4 reshape.107
  12.1 0.0 copy-start.3
  12.1 0.0 copy-start.1
  12.1 0.0 all-reduce.5.cloned.1.call-update
  12.1 0.0 all-gather.3.cloned.1.call-start
  12.2 0.0 copy-done.5
  12.2 0.6 dynamic-slice
  13.8 75.9 %all-reduce.5.cloned.1.call-done = bf16[3648,128]{1,0:T(8,128)(2,1)} async-done(((bf16[3648,128]{1,0:T(8,128)(2,1)}), bf16[3648,128]{1,0:T(8,128)(2,1)}) %all-reduce.5.cloned.1.call-update) | async-done | bytes 933904
  89.7 1.6 convert_multiply_fusion.2
  91.3 1.7 div.28
  92.9 1.8 fusion.13
  94.8 0.0 all-gather.3.cloned.1.call-update
  94.8 0.0 all-gather.5.cloned.1.call-start
  94.8 141.0 %all-gather.3.cloned.1.call-done = bf16[3584,512]{1,0:T(8,128)(2,1)} async-done(((bf16[112,512]{1,0:T(8,128)(2,1)}), bf16[3584,512]{1,0:T(8,128)(2,1)}) %all-gather.3.cloned.1.call-update) | async-done | bytes 3670032 | tf_op jit(solution)/shard_map/all_gather | solution.py:78
  235.8 0.0 all-gather.5.cloned.1.call-update
  235.8 0.0 copy-done.3
  235.9 0.0 copy-done.1
  235.9 0.7 fusion
  236.6 1.7 multiply_cosine_fusion
  238.3 0.9 dynamic-slice_bitcast_fusion
  239.2 0.0 copy-done.4
  239.2 0.5 fusion.12
  239.8 0.2 dynamic-update-slice
  239.9 109.2 %all-reduce.1 = bf16[3584]{0:T(1024)(128)(2,1)S(1)} all-reduce(bf16[3584]{0:T(1024)(128)(2,1)S(1)} %dynamic-update-slice), channel_id=1, replica_groups=mesh['fsdp'=32,'rep'=8] {'fsdp','rep'}, use_global_device_ids=true, to_apply=%add.1 | all-reduce | flops 3584 | bytes 14336
  349.2 176.8 %all-gather.5.cloned.1.call-done = bf16[3584,4096]{1,0:T(8,128)(2,1)} async-done(((bf16[3584,512]{1,0:T(8,128)(2,1)}), bf16[3584,4096]{1,0:T(8,128)(2,1)}) %all-gather.5.cloned.1.call-update) | async-done | bytes 29360144 | tf_op jit(solution)/shard_map/all_gather | solution.py:85
  526.0 19.2 %fusion.3 = f32[480,4096]{1,0:T(8,128)S(1)} fusion(bf16[3584,4096]{1,0:T(8,128)(2,1)} %all-gather.5.cloned.1.call-done, bf16[480,3584]{1,0:T(8,128)(2,1)} %param.6, f32[3584]{0:T(1024)S(1)} %convert_add_fusion, f32[480]{0:T(512)S(1)} %add_rsqrt_fusion), kind=kOutput, calls=%fused_computation.5 | convolution fusion | flops 14099742720 | bytes 40681344 | tf_op jit(solution)/shard_map/dot_general | solution.py:83
  545.2 0.0 copy-start
  545.2 1.5 slice.42
  546.7 2.1 copy-done
  548.9 1.1 slice.62
  550.0 2.2 reshape.110
  552.2 0.0 copy-done.2
  552.2 0.0 slice-start
  552.2 0.5 subtract_convert_fusion.1
  552.7 0.5 pad_maximum_fusion.1
  553.3 1.1 copy.14
  554.4 0.0 slice-done
  554.4 1.8 copy.12
  556.2 0.6 subtract_convert_fusion
  556.9 0.2 pad_maximum_fusion
  557.1 1.9 copy.13
  (7 shorter events, 0.0 us)
Async XLA Ops:
  7.2 5.0 copy-start.5
  7.2 82.5 %all-reduce.5.cloned.1.call-start = ((), (), s32[]{:S(2)}) async-start(), calls=%async_computation.2 | async-start | bytes 1867776
  12.1 223.7 %copy-start.3 = (s32[480]{0:T(512)S(1)}, s32[480]{0:T(512)}, u32[]{:S(2)}) copy-start(s32[480]{0:T(512)} %param.7) | copy-start | bytes 5764
  12.1 223.8 %copy-start.1 = (bf16[480,3584]{1,0:T(8,128)(2,1)S(1)}, bf16[480,3584]{1,0:T(8,128)(2,1)}, u32[]{:S(2)}) copy-start(bf16[480,3584]{1,0:T(8,128)(2,1)} %param.6) | copy-start | bytes 10321924
  12.1 223.7 %all-gather.3.cloned.1.call-start = ((), (), s32[]{:S(2)}) async-start(), calls=%async_computation | async-start | bytes 3784704 | tf_op jit(solution)/shard_map/all_gather | solution.py:78
  94.8 431.2 %all-gather.5.cloned.1.call-start = ((), (), s32[]{:S(2)}) async-start(), calls=%async_computation.1 | async-start | bytes 33030144 | tf_op jit(solution)/shard_map/all_gather | solution.py:85
  235.8 3.5 copy-start.4
  545.2 3.7 copy-start
  550.0 2.2 copy-start.2
  552.2 2.2 slice-start
Sparse Core Ops, SparseCore 0:
  12.2 77.4 all-reduce.4
  94.9 140.8 all-gather.2
  237.6 288.3 all-gather.4
where the time goes:
time: 566 us
  waiting for transfers between devices  394 us (70%)
  blocking collectives  109 us (19%)
  matrix products  19.2 us (3%)
  local copies, waits for them, and re-layouts  18.6 us (3%)
  between operations  14.9 us (3%)
  other arithmetic  9.67 us (2%)
    all_gather x1, waiting for transfers between devices, on_device(): lax.all_gather(column_weight, 'rep', axis=1, tiled=True)  177 us
    all_gather x1, waiting for transfers between devices, on_device(): column_weight = lax.all_gather(own_weight, 'fsdp', axis=0, tiled=True)  141 us
    unnamed x1, blocking collectives  109 us
    unnamed x4, waiting for transfers between devices  76 us
    dot_general x1, matrix products, on_device(): jnp.dot(normed, lax.all_gather(column_weight, 'rep', axis=1, tiled=True),...  19.2 us
  transfers between devices with their start and end apart: 3, of which 3 were waited for; matrix products, arithmetic and copies ran while one was open for 1% of the time, Pallas kernels for 0%

commit v1 on v0

v1 whole, which is shorter than its diff:
```python
import functools
import heapq

import jax
import jax.numpy as jnp
from jax import lax
from jax.experimental import pallas as pl
from jax.experimental.pallas import tpu as pltpu
from jax.sharding import PartitionSpec as P

HEAD = 256
EPSILON = 1e-06
ADVANCE_RATE = 0.5
ROPE_BASE = 10000.0
MESH = pl.DeviceIdType.MESH

RINGS = {"x": 4, "y": 4, "z": 8}
BLOCKS = 128
ROWS = 112
COLS = 512
TOK = 480
WIDTH = 3584
ROUTES = (("xyz", 0, 16), ("yzx", 16, 64), ("xzy", 64, 112))
ROUTE_ORDER = (1, 2, 0)


def reach(ring, sign, parity):
    return ring // 2 if (sign > 0) == (parity % 2 == 0) else ring // 2 - 1


def plan():
    rate, latency = 46.6e3, 2.2
    busy, queue, steps, ids = {}, [], [], {}
    serial = 0

    def push(at, event):
        nonlocal serial
        heapq.heappush(queue, (at, serial, event))
        serial += 1

    def send(at, route, item, axis, sign, outs):
        order, low, high = ROUTES[route]
        size = (high - low) * COLS * 2 * (1 if item[0] == 1 else RINGS[order[0]])
        begin = max(at, busy.get((axis, sign), 0.0))
        busy[axis, sign] = begin + size / rate
        ids[route, item] = len(ids)
        outs.append((item, axis, sign))
        push(busy[axis, sign] + latency, ("item", route, item, sign))

    at = 10.0
    for route in ROUTE_ORDER:
        at += (ROUTES[route][2] - ROUTES[route][1]) / ROWS * 9.8
        push(at, ("own", route, None, 0))
    left = {}
    while queue:
        at, _, (kind, route, item, sign) = heapq.heappop(queue)
        one, two, three = ROUTES[route][0]
        outs = []
        if kind == "own":
            left[route] = RINGS[one] - 1
            for s in (1, -1):
                if reach(RINGS[one], s, route):
                    send(at, route, (1, s, 0), one, s, outs)
        elif item[0] == 1:
            if abs(item[1]) < reach(RINGS[one], sign, route):
                send(at, route, (1, item[1] + sign, 0), one, sign, outs)
            left[route] -= 1
            if left[route] == 0:
                for s in (1, -1):
                    send(at, route, (2, s, 0), two, s, outs)
                for s in (1, -1):
                    send(at, route, (3, 0, s), three, s, outs)
        elif item[0] == 2:
            if abs(item[1]) < reach(RINGS[two], sign, route + 1):
                send(at, route, (2, item[1] + sign, 0), two, sign, outs)
            for s in (1, -1):
                send(at, route, (3, item[1], s), three, s, outs)
        else:
            if abs(item[2]) < reach(RINGS[three], sign, item[1]):
                send(at, route, (3, item[1], item[2] + sign), three, sign, outs)
        steps.append((kind, route, item, outs))
    return steps, ids


def kernel(
    steps, ids,
    tok_in, fast_in, slow_in, gain_in, cos_in, sin_in,
    q_out, k_out, v_out, weight_out, gain_out,
    buf0, buf1, buf2, tok, own1, got1, sum2, got2, slow, fresh, gain, gain_got1, gain_sum, gain_got2, gain_new,
    cosine, sine, turn_c, turn_s, acc, out,
    load_sem, pair_send, pair_recv, rs_send, rs_recv, item_recv, item_send, hand_send, hand_recv, out_sem,
):
    bufs = (buf0, buf1, buf2)
    f = lax.axis_index("fsdp")
    r = lax.axis_index("rep")
    zl, x, y = lax.rem(f, 2), lax.rem(f // 2, 4), f // 8
    zh, c = r // 2, lax.rem(r, 2)
    z = zh * 2 + zl
    at = {"x": x, "y": y, "z": z}

    def device(px, py, pz, pc):
        return ((py * 4 + px) * 2 + lax.rem(pz, 2), (pz // 2) * 2 + pc)

    def wrap(p, off, n):
        return lax.rem(p + (off % n), n)

    def beside(axis, sign):
        p = dict(at)
        p[axis] = wrap(p[axis], sign, RINGS[axis])
        return device(p["x"], p["y"], p["z"], c)

    partner = (f, zh * 2 + 1 - c)
    peers = [(f, wrap(zh, k, 4) * 2 + c) for k in (1, 2, 3)]
    sides = {(a, s): beside(a, s) for a in "xyz" for s in (1, -1)}

    def load(src, dst, sem):
        return pltpu.make_async_copy(src, dst, load_sem.at[sem])

    loads = [
        load(gain_in, gain, 0),
        load(slow_in, slow, 1),
        load(tok_in, tok, 2),
        load(cos_in, cosine, 3),
        load(sin_in, sine, 4),
    ]
    mine = []
    for k in range(4):
        cols = pl.ds(pl.multiple_of((k * 2 + c) * COLS, COLS), COLS)
        mine.append(load(fast_in.at[:, cols], own1.at[k], 5 + k))
    for copy in mine + loads:
        copy.start()

    barrier = pltpu.get_barrier_semaphore()
    everyone = [partner] + peers + list(sides.values())
    for peer in everyone:
        pl.semaphore_signal(barrier, inc=1, device_id=peer, device_id_type=MESH)
    pl.semaphore_wait(barrier, len(everyone))

    def remote(src, dst, send_sem, recv_sem, peer):
        return pltpu.make_async_remote_copy(
            src_ref=src, dst_ref=dst, send_sem=send_sem, recv_sem=recv_sem,
            device_id=peer, device_id_type=MESH,
        )

    pair = []
    for k in range(4):
        cols = pl.ds(pl.multiple_of((k * 2 + 1 - c) * COLS, COLS), COLS)
        pair.append(remote(fast_in.at[:, cols], got1.at[k], pair_send.at[k], pair_recv.at[k], partner))
    loads[0].wait()
    pair.append(remote(gain, gain_got1, pair_send.at[4], pair_recv.at[4], partner))
    for copy in pair:
        copy.start()
    for copy in mine:
        copy.wait()
    for copy in pair:
        copy.wait_recv()
    gain_sum[...] = gain[...] + gain_got1[...]
    for k in (1, 2, 3):
        to = wrap(zh, k, 4)
        sum2[k - 1] = (own1[to].astype(jnp.float32) + got1[to].astype(jnp.float32)).astype(jnp.bfloat16)
    scatter = []
    for n in range(3):
        scatter.append(remote(gain_sum, gain_got2.at[n], rs_send.at[9 + n], rs_recv.at[9 + n], peers[n]))
    for route in ROUTE_ORDER:
        rows = pl.ds(ROUTES[route][1], ROUTES[route][2] - ROUTES[route][1])
        for n in range(3):
            s = route * 3 + n
            scatter.append(
                remote(sum2.at[n, rows], got2.at[n, rows], rs_send.at[s], rs_recv.at[s], peers[n])
            )
    for copy in scatter:
        copy.start()
    loads[1].wait()
    for copy in scatter[:3]:
        copy.wait_recv()
    totals = gain_sum[...] + gain_got2[0] + gain_got2[1] + gain_got2[2]
    old_gain = totals[1:2, :]
    new_gain = old_gain + ADVANCE_RATE * (totals[0:1, :] / 8.0 - old_gain)
    gain_new[...] = jnp.broadcast_to(new_gain, (8, 128))
    scale_row = 1.0 + new_gain.astype(jnp.bfloat16).astype(jnp.float32)
    gain_store = pltpu.make_async_copy(gain_new, gain_out, out_sem.at[8])
    gain_store.start()

    def update(route):
        low, high = ROUTES[route][1:]
        for n in range(3):
            rows = pl.ds(low, high - low)
            remote(
                sum2.at[n, rows], got2.at[n, rows], rs_send.at[route * 3 + n], rs_recv.at[route * 3 + n], peers[n]
            ).wait_recv()
        total = own1[zh, low:high].astype(jnp.float32) + got1[zh, low:high].astype(jnp.float32)
        for n in range(3):
            total = total + got2[n, low:high].astype(jnp.float32)
        old = slow[low:high]
        new = old + ADVANCE_RATE * (total / 8.0 - old)
        fresh[low:high] = new
        shape = (high - low, 128)
        eye = lax.broadcasted_iota(jnp.int32, shape, 0) + low == lax.broadcasted_iota(jnp.int32, shape, 1)
        scale = jnp.sum(jnp.where(eye, jnp.broadcast_to(scale_row, shape), 0.0), axis=1, keepdims=True)
        scaled = new.astype(jnp.bfloat16).astype(jnp.float32) * scale
        bufs[route][c, piece(route, (1, 0, 0))[0]] = scaled.astype(jnp.bfloat16)

    def piece(route, item):
        one, two, three = ROUTES[route][0]
        n1, n2, n3 = RINGS[one], RINGS[two], RINGS[three]
        p1, p2, p3 = at[one], at[two], at[three]
        if item[0] == 1:
            return (p3 * n2 + p2) * n1 + wrap(p1, -item[1], n1), 1
        if item[0] == 2:
            return (p3 * n2 + wrap(p2, -item[1], n2)) * n1, n1
        return (wrap(p3, -item[2], n3) * n2 + wrap(p2, -item[1], n2)) * n1, n1

    def view(route, item):
        start, size = piece(route, item)
        return bufs[route].at[c, pl.ds(start, size)]

    def forward(route, item, axis, sign):
        phase, a, b = item
        held = (phase, a - sign, b) if phase < 3 else (phase, a, b - sign)
        part = view(route, held)
        remote(part, part, item_send.at[route], item_recv.at[ids[route, item]], sides[axis, sign]).start()

    def hand(route, item):
        part = view(route, item)
        remote(part, part, hand_send.at[route], hand_recv.at[route], partner).start()

    def tables():
        loads[2].wait()
        loads[3].wait()
        loads[4].wait()

        def rows_of(i, _):
            rows = pl.ds(pl.multiple_of(i * 16, 16), 16)
            t = tok[rows, :].astype(jnp.float32)
            inv = lax.rsqrt(jnp.sum(t * t, axis=1, keepdims=True) * (1.0 / WIDTH) + EPSILON)
            turn_c[0, rows, :] = cosine[rows, :] * inv
            turn_s[0, rows, :] = sine[rows, :] * inv
            turn_c[1, rows, :] = jnp.broadcast_to(inv, (16, 128))
            turn_s[1, rows, :] = jnp.zeros((16, 128), jnp.float32)
            return 0

        lax.fori_loop(0, TOK // 16, rows_of, 0)

    started = 0
    for kind, route, item, outs in steps:
        if kind == "own":
            update(route)
            item = (1, 0, 0)
        else:
            part = view(route, item)
            remote(part, part, item_send.at[route], item_recv.at[ids[route, item]], partner).wait_recv()
        for target, axis, sign in outs:
            forward(route, target, axis, sign)
        hand(route, item)
        if kind == "own":
            started += 1
            if started == 3:
                weight_store = pltpu.make_async_copy(fresh, weight_out, out_sem.at[9])
                weight_store.start()
                tables()

    for route in range(3):
        other = bufs[route].at[1 - c]
        remote(other, other, hand_send.at[route], hand_recv.at[route], partner).wait_recv()

    def columns(b, _):
        bz, bc = b // 2, lax.rem(b, 2)
        parts = []
        for py in range(4):
            for px in range(4):
                for pz in range(2):
                    wz = bz * 2 + pz
                    parts.append(buf0[bc, (wz * 4 + py) * 4 + px])
                    parts.append(buf1[bc, (px * 8 + wz) * 4 + py])
                    parts.append(buf2[bc, (py * 8 + wz) * 4 + px])
        acc[...] = jnp.dot(tok[...], jnp.concatenate(parts, axis=0), preferred_element_type=jnp.float32)
        kind = b // 6
        for h in range(0, COLS, HEAD):
            u, w = acc[:, h : h + 128], acc[:, h + 128 : h + 256]
            tc, ts = turn_c[kind], turn_s[kind]
            out[b, :, h : h + 128] = (u * tc - w * ts).astype(jnp.bfloat16)
            out[b, :, h + 128 : h + 256] = (w * tc + u * ts).astype(jnp.bfloat16)

        def put(ref, first):
            cols = pl.ds(pl.multiple_of((b - first) * COLS, COLS), COLS)
            pltpu.make_async_copy(out.at[b], ref.at[:, cols], out_sem.at[b]).start()

        @pl.when(b < 4)
        def _():
            put(q_out, 0)

        @pl.when((b >= 4) & (b < 6))
        def _():
            put(k_out, 4)

        @pl.when(b >= 6)
        def _():
            put(v_out, 6)

        return 0

    lax.fori_loop(0, 8, columns, 0)

    for copy in pair + scatter:
        copy.wait_send()
    for route in range(3):
        most = bufs[route].at[0, pl.ds(0, BLOCKS - 1)]
        remote(most, most, item_send.at[route], item_recv.at[0], partner).wait_send()
        every = bufs[route].at[0]
        remote(every, every, hand_send.at[route], hand_recv.at[route], partner).wait_send()
    gain_store.wait()
    weight_store.wait()
    for b in range(8):
        ref, first = ((q_out, 0), (k_out, 4), (v_out, 6))[(b >= 4) + (b >= 6)]
        pltpu.make_async_copy(out.at[b], ref.at[:, pl.ds((b - first) * COLS, COLS)], out_sem.at[b]).wait()


def on_device(tokens, positions, slow_weight, fast_weight, slow_gain, fast_gain):
    steps, ids = plan()
    r = lax.axis_index("rep")
    half = HEAD // 2
    rates = ROPE_BASE ** (-(jnp.arange(half, dtype=jnp.float32) * 2.0 / HEAD))
    angles = positions.astype(jnp.float32)[:, None] * rates[None, :]
    placed = lax.dynamic_update_slice(jnp.zeros((128,), jnp.float32), slow_gain, (r * 14,))
    fast_row = jnp.pad(fast_gain.astype(jnp.float32), ((0, 0), (0, 128 - ROWS)))
    gains = jnp.concatenate([fast_row, placed[None], jnp.zeros((6, 128), jnp.float32)], axis=0)
    f32, bf16 = jnp.float32, jnp.bfloat16
    vmem, dma = pltpu.VMEM, pltpu.SemaphoreType.DMA
    anywhere = pl.BlockSpec(memory_space=pl.ANY)
    q, k, v, new_weight, new_gain = pl.pallas_call(
        functools.partial(kernel, steps, ids),
        out_shape=(
            jax.ShapeDtypeStruct((TOK, 2048), bf16),
            jax.ShapeDtypeStruct((TOK, 1024), bf16),
            jax.ShapeDtypeStruct((TOK, 1024), bf16),
            jax.ShapeDtypeStruct((ROWS, COLS), f32),
            jax.ShapeDtypeStruct((8, 128), f32),
        ),
        in_specs=[anywhere] * 6,
        out_specs=(anywhere,) * 5,
        scratch_shapes=[
            *(vmem((2, BLOCKS, high - low, COLS), bf16) for _, low, high in ROUTES),
            vmem((TOK, WIDTH), bf16),
            vmem((4, ROWS, COLS), bf16),
            vmem((4, ROWS, COLS), bf16),
            vmem((3, ROWS, COLS), bf16),
            vmem((3, ROWS, COLS), bf16),
            vmem((ROWS, COLS), f32),
            vmem((ROWS, COLS), f32),
            vmem((8, 128), f32),
            vmem((8, 128), f32),
            vmem((8, 128), f32),
            vmem((3, 8, 128), f32),
            vmem((8, 128), f32),
            vmem((TOK, 128), f32),
            vmem((TOK, 128), f32),
            vmem((2, TOK, 128), f32),
            vmem((2, TOK, 128), f32),
            vmem((TOK, COLS), f32),
            vmem((8, TOK, COLS), bf16),
            dma((9,)),
            dma((5,)),
            dma((5,)),
            dma((12,)),
            dma((12,)),
            dma((len(ids),)),
            dma((3,)),
            dma((3,)),
            dma((3,)),
            dma((10,)),
        ],
        compiler_params=pltpu.CompilerParams(
            collective_id=0, has_side_effects=True, vmem_limit_bytes=60 * 1024 * 1024
        ),
    )(tokens, fast_weight[0], slow_weight, gains, jnp.cos(angles), jnp.sin(angles))
    return q, k, v, new_weight, lax.dynamic_slice(new_gain[0], (r * 14,), (14,))


def solution(mesh):
    return jax.shard_map(
        on_device,
        mesh=mesh,
        in_specs=(
            P(("fsdp", "rep"), None),
            P(("fsdp", "rep")),
            P("fsdp", "rep"),
            P("rep", "fsdp", None),
            P(("fsdp", "rep")),
            P("rep", "fsdp"),
        ),
        out_specs=(
            P(("fsdp", "rep"), None),
            P(("fsdp", "rep"), None),
            P(("fsdp", "rep"), None),
            P("fsdp", "rep"),
            P(("fsdp", "rep")),
        ),
        check_vma=False,
    )
```

time: 566 us -> 127 us (0.22)
  the two profiles are of different devices: /device:TPU:35 before, /device:TPU:1 now
where the time goes in v1:
time: 127 us
  Pallas kernels  114 us (90%)
  local copies, waits for them, and re-layouts  7.98 us (6%)
  other arithmetic  3.76 us (3%)
    pallas_call x1, Pallas kernels, on_device(): pl.pallas_call(functools.partial(kernel, steps, ids), out_shape=(jax.Shap...  114 us
    unnamed x10, local copies, waits for them, and re-layouts  5.77 us

profile of v1, /device:TPU:1, one launch (start us, length us, event | category | flops | bytes accessed | tf_op | source)
XLA Modules:
  0.0 126.5 jit_solution(6617332151639567155)
XLA Ops:
  0.6 0.9 dynamic_update_slice.4
  1.5 0.1 pad.11.clone
  1.6 0.7 pad_convert_fusion
  2.3 0.7 maximum_maximum_fusion.gain_in
  2.9 0.7 convert_element_type.6
  3.6 1.7 %multiply_sine_fusion = (f32[480,128]{1,0:T(8,128)}, f32[480,128]{1,0:T(8,128)}) fusion(f32[128]{0:T(128)S(1)} %negate_power_fusion, f32[480]{0:T(512)S(1)} %convert_element_type.6), kind=kLoop, calls=%fused_computation | loop fusion | flops 61440 | bytes 493952 | tf_op jit(solution)/shard_map/sin | solution.py:375
  5.4 114.1 %shard_map.101 = (bf16[480,2048]{1,0:T(8,128)(2,1)}, bf16[480,1024]{1,0:T(8,128)(2,1)}, bf16[480,1024]{1,0:T(8,128)(2,1)}, f32[112,512]{1,0:T(8,128)}, f32[8,128]{1,0:T(8,128)}) custom-call(bf16[480,3584]{1,0:T(8,128)(2,1)} %tok_in.1, bf16[112,4096]{1,0:T(8,128)(2,1)} %bitcast.4, f32[112,512]{1,0:T(8,128)} %slow_in.1, f32[8,128]{1,0:T(8,128)} %maximum_maximum_fusion.gain_in, ...), custom_call_target="tpu_custom_call" | custom-call | tf_op jit(solution)/shard_map/pallas_call | solution.py:330
  119.5 0.7 slice.3
  120.2 0.6 dynamic-slice_bitcast_fusion
  120.7 0.0 copy-start.1
  120.7 0.0 copy-start
  120.8 3.2 %copy.16 = bf16[480,2048]{1,0:T(8,128)(2,1)} copy(bf16[480,2048]{1,0:T(8,128)(2,1)} %get-tuple-element.22) | data formatting | bytes 3932160
  123.9 0.0 copy-done.1
  123.9 0.0 copy-start.2
  123.9 0.9 copy.17
  124.9 0.0 copy-done
  124.9 0.9 copy.18
  125.8 0.0 copy-done.2
  125.8 0.7 copy.19
  (3 shorter events, 0.0 us)
Async XLA Ops:
  120.7 3.2 %copy-start.1 = (bf16[480,1024]{1,0:T(8,128)(2,1)S(1)}, bf16[480,1024]{1,0:T(8,128)(2,1)}, u32[]{:S(2)}) copy-start(bf16[480,1024]{1,0:T(8,128)(2,1)} %get-tuple-element.23) | copy-start | bytes 2949124
  120.7 4.1 %copy-start = (bf16[480,1024]{1,0:T(8,128)(2,1)S(1)}, bf16[480,1024]{1,0:T(8,128)(2,1)}, u32[]{:S(2)}) copy-start(bf16[480,1024]{1,0:T(8,128)(2,1)} %get-tuple-element.24) | copy-start | bytes 2949124
  123.9 1.9 %copy-start.2 = (f32[112,512]{1,0:T(8,128)S(1)}, f32[112,512]{1,0:T(8,128)}, u32[]{:S(2)}) copy-start(f32[112,512]{1,0:T(8,128)} %get-tuple-element.25) | copy-start | bytes 688132

commit v2 on v1

v2 whole, which is shorter than its diff:
```python
import functools
import heapq

import jax
import jax.numpy as jnp
from jax import lax
from jax.experimental import pallas as pl
from jax.experimental.pallas import tpu as pltpu
from jax.sharding import PartitionSpec as P

HEAD = 256
EPSILON = 1e-06
ADVANCE_RATE = 0.5
LOG_BASE = 9.210340371976184
MESH = pl.DeviceIdType.MESH

RINGS = {"x": 4, "y": 4, "z": 8}
BLOCKS = 128
ROWS = 112
COLS = 512
TOK = 480
WIDTH = 3584
ROUTES = (("xyz", 0, 16), ("yzx", 16, 32), ("yzx", 32, 64), ("xzy", 64, 80), ("xzy", 80, 112))
ROUTE_ORDER = (3, 1, 4, 2, 0)
NR = len(ROUTES)
GROUPS = ((1, 3), (0, 2, 4))
HAND_TIME = 2.5
HALF_K = WIDTH // 2
STRIPS = ((0, 0, 2), (1, 0, 2), (2, 0, 1), (2, 1, 1), (3, 0, 2), (4, 0, 1), (4, 1, 1))
TABLE_ROWS = ((0, 128), (128, 128), (256, 128), (384, 96))


def reach(ring, sign, parity):
    return ring // 2 if (sign > 0) == (parity % 2 == 0) else ring // 2 - 1


def distance(route, item):
    place = ROUTES[route][0].index("z")
    if item[0] <= place:
        return 0
    return item[place] % 8


def plan():
    rate, latency = 46.6e3, 2.2
    busy, queue, events, ids = {}, [], [], {}
    serial = 0

    def push(at, event):
        nonlocal serial
        heapq.heappush(queue, (at, serial, event))
        serial += 1

    def send(at, route, item, axis, sign, outs):
        order, low, high = ROUTES[route]
        size = (high - low) * COLS * 2 * (1 if item[0] == 1 else RINGS[order[0]])
        begin = max(at, busy.get((axis, sign), 0.0))
        busy[axis, sign] = begin + size / rate
        ids[route, item] = len(ids)
        outs.append((item, axis, sign))
        push(busy[axis, sign] + latency, ("item", route, item, sign))

    at = 10.0
    for route in ROUTE_ORDER:
        at += (ROUTES[route][2] - ROUTES[route][1]) / ROWS * 9.8
        push(at, ("own", route, None, 0))
    left = {}
    ready = {}
    while queue:
        at, _, (kind, route, item, sign) = heapq.heappop(queue)
        one, two, three = ROUTES[route][0]
        outs = []
        if kind == "own":
            left[route] = RINGS[one] - 1
            for s in (1, -1):
                if reach(RINGS[one], s, route):
                    send(at, route, (1, s, 0), one, s, outs)
        elif item[0] == 1:
            if abs(item[1]) < reach(RINGS[one], sign, route):
                send(at, route, (1, item[1] + sign, 0), one, sign, outs)
            left[route] -= 1
            if left[route] == 0:
                for s in (1, -1):
                    send(at, route, (2, s, 0), two, s, outs)
                for s in (1, -1):
                    send(at, route, (3, 0, s), three, s, outs)
        elif item[0] == 2:
            if abs(item[1]) < reach(RINGS[two], sign, route + 1):
                send(at, route, (2, item[1] + sign, 0), two, sign, outs)
            for s in (1, -1):
                send(at, route, (3, item[1], s), three, s, outs)
        else:
            if abs(item[2]) < reach(RINGS[three], sign, item[1]):
                send(at, route, (3, item[1], item[2] + sign), three, sign, outs)
        z = distance(route, item or (1, 0, 0))
        ready[route, z] = at
        events.append((at, (kind, route, item, outs)))

    fill = [("strip", n, 1.2) for n in range(len(STRIPS))]
    fill += [("table", n, 0.8) for n in range(len(TABLE_ROWS))]
    units = sorted((max(ready[route, z] for route in group), group, z) for group in GROUPS for z in range(8))
    ends = {}
    for far, need in ((0, (0, 1, 7)), (1, (1, 2, 3)), (3, (5, 6, 7)), (2, (3, 4, 5))):
        ends.setdefault(max(n for n, u in enumerate(units) if u[2] in need), []).append(far)
    work = []
    for n, (when, group, z) in enumerate(units):
        work.append((("unit", group, z), 0.5 * len(group), when))
        work += [(("finish", far), 0.8, when) for far in ends.get(n, ())]
    steps = []
    clock = 8.5
    for at, event in events:
        while fill and at - clock >= 0.6 * fill[0][2]:
            steps.append(fill[0][:2])
            clock += fill.pop(0)[2]
        while work and not fill and work[0][2] < at and work[0][2] + HAND_TIME <= max(clock, at):
            steps.append(work[0][0])
            clock = max(clock, work[0][2] + HAND_TIME) + work.pop(0)[1]
        clock = max(clock, at) + 0.12
        steps.append(event)
    steps += [entry[:2] for entry in fill] + [entry[0] for entry in work]
    return steps, ids


def kernel(
    steps, ids,
    tok_in, fast_in, slow_in, fast_gain_in, slow_gain_in, pos_in,
    q_out, k_out, v_out, weight_out, gain_out,
    *rest,
):
    bufs, rest = rest[:NR], rest[NR:]
    (
        tok, perm, strips, acc, own1, got1, sum2, got2, slow, fast_gain, slow_gain, pos,
        gain, gain_got1, gain_sum, gain_got2, gain_new, turn_c, turn_s, scale,
        load_sem, pair_send, pair_recv, rs_send, rs_recv, item_recv, item_send, hand_send, hand_recv,
    ) = rest
    f = lax.axis_index("fsdp")
    r = lax.axis_index("rep")
    zl, x, y = lax.rem(f, 2), lax.rem(f // 2, 4), f // 8
    zh, c = r // 2, lax.rem(r, 2)
    z = zh * 2 + zl
    at = {"x": x, "y": y, "z": z}

    def device(px, py, pz, pc):
        return ((py * 4 + px) * 2 + lax.rem(pz, 2), (pz // 2) * 2 + pc)

    def wrap(p, off, n):
        return lax.rem(p + (off % n), n)

    def beside(axis, sign):
        p = dict(at)
        p[axis] = wrap(p[axis], sign, RINGS[axis])
        return device(p["x"], p["y"], p["z"], c)

    partner = (f, zh * 2 + 1 - c)
    peers = [(f, wrap(zh, k, 4) * 2 + c) for k in (1, 2, 3)]
    sides = {(a, s): beside(a, s) for a in "xyz" for s in (1, -1)}

    def load(src, dst, sem):
        return pltpu.make_async_copy(src, dst, load_sem.at[sem])

    loads = [
        load(fast_gain_in, fast_gain, 0),
        load(slow_gain_in, slow_gain.at[0:1], 1),
        load(slow_in, slow, 2),
        load(pos_in, pos, 3),
        load(tok_in, tok, 4),
    ]
    mine = []
    for k in range(4):
        cols = pl.ds(pl.multiple_of((k * 2 + c) * COLS, COLS), COLS)
        mine.append(load(fast_in.at[:, cols], own1.at[k], 5 + k))
    barrier = pltpu.get_barrier_semaphore()
    everyone = [partner] + peers + list(sides.values())
    for peer in everyone:
        pl.semaphore_signal(barrier, inc=1, device_id=peer, device_id_type=MESH)
    for copy in loads[:2] + mine + loads[2:]:
        copy.start()

    def clear(b, _):
        acc[b] = jnp.zeros((TOK, COLS), jnp.float32)
        return 0

    lax.fori_loop(0, 8, clear, 0)
    for copy in loads[:2]:
        copy.wait()
    lanes = lax.broadcasted_iota(jnp.int32, (8, 128), 1)
    gain[...] = jnp.where(lanes < 14, slow_gain[...], 0.0)
    gain[...] = pltpu.roll(gain[...], r * 14, 1)
    gain[1:2, :] = gain[0:1, :]
    gain[0:1, :] = jnp.zeros((1, 128), jnp.float32)
    gain[0:1, 0:ROWS] = fast_gain[...].astype(jnp.float32)
    pl.semaphore_wait(barrier, len(everyone))

    def remote(src, dst, send_sem, recv_sem, peer):
        return pltpu.make_async_remote_copy(
            src_ref=src, dst_ref=dst, send_sem=send_sem, recv_sem=recv_sem,
            device_id=peer, device_id_type=MESH,
        )

    pair = []
    for k in range(4):
        cols = pl.ds(pl.multiple_of((k * 2 + 1 - c) * COLS, COLS), COLS)
        pair.append(remote(fast_in.at[:, cols], got1.at[k], pair_send.at[k], pair_recv.at[k], partner))
    pair.append(remote(gain, gain_got1, pair_send.at[4], pair_recv.at[4], partner))
    for copy in pair:
        copy.start()
    for copy in mine:
        copy.wait()
    for copy in pair:
        copy.wait_recv()
    gain_sum[...] = gain[...] + gain_got1[...]
    for k in (1, 2, 3):
        to = wrap(zh, k, 4)
        sum2[k - 1] = (own1[to].astype(jnp.float32) + got1[to].astype(jnp.float32)).astype(jnp.bfloat16)
    scatter = []
    for n in range(3):
        s = NR * 3 + n
        scatter.append(remote(gain_sum, gain_got2.at[n], rs_send.at[s], rs_recv.at[s], peers[n]))
    for route in ROUTE_ORDER:
        rows = pl.ds(ROUTES[route][1], ROUTES[route][2] - ROUTES[route][1])
        for n in range(3):
            s = route * 3 + n
            scatter.append(
                remote(sum2.at[n, rows], got2.at[n, rows], rs_send.at[s], rs_recv.at[s], peers[n])
            )
    for copy in scatter:
        copy.start()

    def gains():
        loads[2].wait()
        for copy in scatter[:3]:
            copy.wait_recv()
        totals = gain_sum[...] + gain_got2[0] + gain_got2[1] + gain_got2[2]
        old_gain = totals[1:2, :]
        new_gain = old_gain + ADVANCE_RATE * (totals[0:1, :] / 8.0 - old_gain)
        row = 1.0 + new_gain.astype(jnp.bfloat16).astype(jnp.float32)
        eye = lax.broadcasted_iota(jnp.int32, (ROWS, 128), 0) == lax.broadcasted_iota(jnp.int32, (ROWS, 128), 1)
        column = jnp.sum(jnp.where(eye, jnp.broadcast_to(row, (ROWS, 128)), 0.0), axis=1, keepdims=True)
        scale[...] = jnp.broadcast_to(column, (ROWS, 128))
        gain_new[...] = jnp.broadcast_to(new_gain, (8, 128))
        gain_new[...] = pltpu.roll(gain_new[...], lax.rem(128 - r * 14, 128), 1)
        gain_out[...] = gain_new[0:1, 0:14]

    def update(route):
        low, high = ROUTES[route][1:]
        for n in range(3):
            rows = pl.ds(low, high - low)
            remote(
                sum2.at[n, rows], got2.at[n, rows], rs_send.at[route * 3 + n], rs_recv.at[route * 3 + n], peers[n]
            ).wait_recv()
        total = own1[zh, low:high].astype(jnp.float32) + got1[zh, low:high].astype(jnp.float32)
        for n in range(3):
            total = total + got2[n, low:high].astype(jnp.float32)
        old = slow[low:high]
        new = old + ADVANCE_RATE * (total / 8.0 - old)
        weight_out[low:high] = new
        scaled = new.astype(jnp.bfloat16).astype(jnp.float32) * jnp.tile(scale[low:high], (1, COLS // 128))
        bufs[route][c, piece(route, (1, 0, 0))[0]] = scaled.astype(jnp.bfloat16)

    def spot(route, px, py, pz):
        one, two, three = ROUTES[route][0]
        p = {"x": px, "y": py, "z": pz}
        return (p[three] * RINGS[two] + p[two]) * RINGS[one] + p[one]

    def piece(route, item):
        one, two, three = ROUTES[route][0]
        n1, n2, n3 = RINGS[one], RINGS[two], RINGS[three]
        p1, p2, p3 = at[one], at[two], at[three]
        if item[0] == 1:
            return (p3 * n2 + p2) * n1 + wrap(p1, -item[1], n1), 1
        if item[0] == 2:
            return (p3 * n2 + wrap(p2, -item[1], n2)) * n1, n1
        return (wrap(p3, -item[2], n3) * n2 + wrap(p2, -item[1], n2)) * n1, n1

    def view(route, item):
        start, size = piece(route, item)
        return bufs[route].at[c, pl.ds(start, size)]

    def forward(route, item, axis, sign):
        phase, a, b = item
        held = (phase, a - sign, b) if phase < 3 else (phase, a, b - sign)
        part = view(route, held)
        remote(part, part, item_send.at[route], item_recv.at[ids[route, item]], sides[axis, sign]).start()

    def hand(route, item):
        part = view(route, item)
        sem = hand_recv.at[route * 8 + distance(route, item)]
        remote(part, part, hand_send.at[route], sem, partner).start()

    def table(first, count):
        rows = pl.ds(first, count)
        spots = jnp.broadcast_to(pos[0:1, first : first + count].astype(jnp.float32), (count, count))
        eye = lax.broadcasted_iota(jnp.int32, (count, count), 0) == lax.broadcasted_iota(jnp.int32, (count, count), 1)
        place = jnp.sum(jnp.where(eye, spots, 0.0), axis=1, keepdims=True)
        lane = lax.broadcasted_iota(jnp.int32, (1, 128), 1).astype(jnp.float32)
        rates = jnp.exp(lane * (-2.0 / HEAD * LOG_BASE))
        angles = place * rates
        t = tok[rows, :].astype(jnp.float32)
        inv = lax.rsqrt(jnp.sum(t * t, axis=1, keepdims=True) * (1.0 / WIDTH) + EPSILON)
        turn_c[0, rows, :] = jnp.cos(angles) * inv
        turn_s[rows, :] = jnp.sin(angles) * inv
        turn_c[1, rows, :] = jnp.broadcast_to(inv, (count, 128))

    def strip(n):
        route, parity, parities = STRIPS[n]
        low, high = ROUTES[route][1:]
        tall = high - low
        lane = lax.broadcasted_iota(jnp.int32, (1, 256), 1)
        if parities == 2:
            pz, lane = lane // 128, lax.rem(lane, 128)
        else:
            pz = parity
        source = (lane // tall) * (2 * ROWS) + pz * ROWS + low + lax.rem(lane, tall)

        def rows_of(i, _):
            first = pl.multiple_of(i * 128, 128)
            k = lax.broadcasted_iota(jnp.int32, (128, 256), 0) + first
            perm[pl.ds(first, 128), :] = jnp.where(k == source, 1.0, 0.0).astype(jnp.bfloat16)
            return 0

        lax.fori_loop(0, HALF_K // 128, rows_of, 0)
        for p in range(2):
            moved = jnp.dot(
                tok[:, HALF_K * p : HALF_K * (p + 1)], perm[...], preferred_element_type=jnp.float32
            ).astype(jnp.bfloat16)
            to = 16 * low + p * 8 * tall
            if parities == 2:
                strips[0, :, to : to + 128] = moved[:, :128]
                strips[1, :, to : to + 128] = moved[:, 128:]
            else:
                strips[parity, :, to : to + 256] = moved

    def unit(group, far):
        for route in group:
            some = bufs[route].at[1 - c, pl.ds(0, 16)]
            remote(some, some, hand_send.at[route], hand_recv.at[route * 8 + far], partner).wait_recv()
        wz = wrap(z, -far, 8)

        def of_core(bc, _):
            parts = [
                bufs[route][bc, spot(route, px, py, wz)] for route in group for py in range(4) for px in range(4)
            ]
            lanes = [
                strips[lax.rem(wz, 2), :, 16 * ROUTES[route][1] : 16 * ROUTES[route][2]] for route in group
            ]
            acc[(wz // 2) * 2 + bc] += jnp.dot(
                jnp.concatenate(lanes, axis=1), jnp.concatenate(parts, axis=0), preferred_element_type=jnp.float32
            )
            return 0

        lax.fori_loop(0, 2, of_core, 0)

    def finish(far):
        bz = wrap(zh, -far, 4)

        def of_core(bc, _):
            b = bz * 2 + bc

            def turned(ref, first):
                start = (b - first) * COLS
                for h in range(0, COLS, HEAD):
                    u, w = acc[b, :, h : h + 128], acc[b, :, h + 128 : h + 256]
                    tc, ts = turn_c[0], turn_s[...]
                    ref[:, pl.ds(pl.multiple_of(start + h, 128), 128)] = (u * tc - w * ts).astype(jnp.bfloat16)
                    ref[:, pl.ds(pl.multiple_of(start + h + 128, 128), 128)] = (w * tc + u * ts).astype(jnp.bfloat16)

            @pl.when(b < 4)
            def _():
                turned(q_out, 0)

            @pl.when((b >= 4) & (b < 6))
            def _():
                turned(k_out, 4)

            @pl.when(b >= 6)
            def _():
                for h in range(0, COLS, 128):
                    cols = pl.ds(pl.multiple_of((b - 6) * COLS + h, 128), 128)
                    v_out[:, cols] = (acc[b, :, h : h + 128] * turn_c[1]).astype(jnp.bfloat16)

            return 0

        lax.fori_loop(0, 2, of_core, 0)

    first_strip, first_table, first_own = True, True, True
    for step in steps:
        if step[0] == "strip":
            if first_strip:
                loads[4].wait()
                first_strip = False
            strip(step[1])
        elif step[0] == "table":
            if first_table:
                loads[3].wait()
                first_table = False
            table(*TABLE_ROWS[step[1]])
        elif step[0] == "unit":
            unit(*step[1:])
        elif step[0] == "finish":
            finish(step[1])
        else:
            kind, route, item, outs = step
            if kind == "own":
                if first_own:
                    gains()
                    first_own = False
                update(route)
                item = (1, 0, 0)
            else:
                part = view(route, item)
                remote(part, part, item_send.at[route], item_recv.at[ids[route, item]], partner).wait_recv()
            for target, axis, sign in outs:
                forward(route, target, axis, sign)
            hand(route, item)

    for copy in pair + scatter:
        copy.wait_send()
    for route in range(NR):
        most = bufs[route].at[0, pl.ds(0, BLOCKS - 1)]
        remote(most, most, item_send.at[route], item_recv.at[0], partner).wait_send()
        every = bufs[route].at[0]
        remote(every, every, hand_send.at[route], hand_recv.at[0], partner).wait_send()


def flush(*refs):
    sem = refs[-1]
    count = len(refs) // 2
    copies = [pltpu.make_async_copy(refs[n], refs[count + n], sem.at[n]) for n in range(count)]
    for copy in copies:
        copy.start()
    for copy in copies:
        copy.wait()


def on_device(tokens, positions, slow_weight, fast_weight, slow_gain, fast_gain):
    steps, ids = plan()
    f32, bf16 = jnp.float32, jnp.bfloat16
    vmem, dma = pltpu.VMEM, pltpu.SemaphoreType.DMA
    shapes = (
        ((TOK, 2048), bf16),
        ((TOK, 1024), bf16),
        ((TOK, 1024), bf16),
        ((ROWS, COLS), f32),
        ((1, 14), f32),
    )
    held = pl.BlockSpec(memory_space=pltpu.VMEM)
    far = pl.BlockSpec(memory_space=pltpu.HBM)
    results = pl.pallas_call(
        functools.partial(kernel, steps, ids),
        out_shape=tuple(vmem(*s) for s in shapes),
        in_specs=[far] * 6,
        out_specs=(held,) * 5,
        scratch_shapes=[
            *(vmem((2, BLOCKS, high - low, COLS), bf16) for _, low, high in ROUTES),
            vmem((TOK, WIDTH), bf16),
            vmem((HALF_K, 256), bf16),
            vmem((2, TOK, HALF_K), bf16),
            vmem((8, TOK, COLS), f32),
            vmem((4, ROWS, COLS), bf16),
            vmem((4, ROWS, COLS), bf16),
            vmem((3, ROWS, COLS), bf16),
            vmem((3, ROWS, COLS), bf16),
            vmem((ROWS, COLS), f32),
            vmem((1, ROWS), bf16),
            vmem((8, 128), f32),
            vmem((1, TOK), jnp.int32),
            vmem((8, 128), f32),
            vmem((8, 128), f32),
            vmem((8, 128), f32),
            vmem((3, 8, 128), f32),
            vmem((8, 128), f32),
            vmem((2, TOK, 128), f32),
            vmem((TOK, 128), f32),
            vmem((ROWS, 128), f32),
            dma((9,)),
            dma((5,)),
            dma((5,)),
            dma((NR * 3 + 3,)),
            dma((NR * 3 + 3,)),
            dma((len(ids),)),
            dma((NR,)),
            dma((NR,)),
            dma((NR * 8,)),
        ],
        compiler_params=pltpu.CompilerParams(
            collective_id=0, has_side_effects=True, vmem_limit_bytes=57 * 1024 * 1024
        ),
    )(
        tokens, fast_weight[0], slow_weight, fast_gain,
        jnp.pad(slow_gain.reshape(1, 14), ((0, 0), (0, 114))), positions.reshape(1, TOK),
    )
    q, k, v, new_weight, new_gain = pl.pallas_call(
        flush,
        out_shape=tuple(jax.ShapeDtypeStruct(*s) for s in shapes),
        in_specs=[held] * 5,
        out_specs=(far,) * 5,
        scratch_shapes=[dma((5,))],
        compiler_params=pltpu.CompilerParams(vmem_limit_bytes=1024 * 1024),
    )(*results)
    return q, k, v, new_weight, new_gain.reshape(14)


def solution(mesh):
    return jax.shard_map(
        on_device,
        mesh=mesh,
        in_specs=(
            P(("fsdp", "rep"), None),
            P(("fsdp", "rep")),
            P("fsdp", "rep"),
            P("rep", "fsdp", None),
            P(("fsdp", "rep")),
            P("rep", "fsdp"),
        ),
        out_specs=(
            P(("fsdp", "rep"), None),
            P(("fsdp", "rep"), None),
            P(("fsdp", "rep"), None),
            P("fsdp", "rep"),
            P(("fsdp", "rep")),
        ),
        check_vma=False,
    )
```

time: 127 us -> 101 us (0.80)
  Pallas kernels: 114 us -> 99.2 us
  local copies, waits for them, and re-layouts: 7.98 us -> 1.17 us
  other arithmetic: 3.76 us -> 0 us
    pallas_call x1 -> x2, Pallas kernels: 114 us -> 99.2 us  [the longest x1 97.1 us: on_device(): pl.pallas_call(functools.partial(kernel, steps, ids), out_shape=tuple((vm...]
    unnamed x10 -> x0, local copies, waits for them, and re-layouts: 5.77 us -> none
    sin x1 -> x0, other arithmetic: 1.74 us -> none  [on_device(): jnp.sin(angles)]
where the time goes in v2:
time: 101 us
  Pallas kernels  99.2 us (98%)
  local copies, waits for them, and re-layouts  1.17 us (1%)
    pallas_call x1, Pallas kernels, on_device(): pl.pallas_call(functools.partial(kernel, steps, ids), out_shape=tuple((vm...  97.1 us
    pallas_call x1, Pallas kernels, on_device(): pl.pallas_call(flush, out_shape=tuple((jax.ShapeDtypeStruct(*s) for s in...  2.03 us

profile of v2, /device:TPU:1, one launch (start us, length us, event | category | flops | bytes accessed | tf_op | source)
XLA Modules:
  0.0 101.1 jit_solution(13166814375391913668)
XLA Ops:
  0.6 1.2 %pad.4.slow_gain_in = f32[1,128]{1,0:T(1,128)} pad(f32[1,14]{1,0:T(1,128)} %bitcast.6, f32[]{:T(128)} %constant.2.clone.1), padding=0_0x0_114 | pad | bytes 572 | tf_op jit(solution)/shard_map/jit(_pad)/pad | solution.py:490
  1.8 97.1 %shard_map.101 = (bf16[480,2048]{1,0:T(8,128)(2,1)S(1)}, bf16[480,1024]{1,0:T(8,128)(2,1)S(1)}, bf16[480,1024]{1,0:T(8,128)(2,1)S(1)}, f32[112,512]{1,0:T(8,128)S(1)}, f32[1,14]{1,0:T(1,128)S(1)}) custom-call(bf16[480,3584]{1,0:T(8,128)(2,1)} %tok_in.1, bf16[112,4096]{1,0:T(8,128)(2,1)} %bitcast.4, f32[112,512]{1,0:T(8,128)} %slow_in.1, ...), custom_call_target="tpu_custom_call" | custom-call | tf_op jit(solution)/shard_map/pallas_call | solution.py:448
  99.0 2.0 %shard_map.102 = (bf16[480,2048]{1,0:T(8,128)(2,1)}, bf16[480,1024]{1,0:T(8,128)(2,1)}, bf16[480,1024]{1,0:T(8,128)(2,1)}, f32[112,512]{1,0:T(8,128)}, f32[1,14]{1,0:T(1,128)}) custom-call(bf16[480,2048]{1,0:T(8,128)(2,1)S(1)} %get-tuple-element.15.refs_0_, bf16[480,1024]{1,0:T(8,128)(2,1)S(1)} %get-tuple-element.16.refs_1_, ...), custom_call_target="tpu_custom_call" | custom-call | tf_op jit(solution)/shard_map/pallas_call | solution.py:492

commit v3 on v2

--- a/solution.py
+++ b/solution.py
@@ -23,7 +23,7 @@
 ROUTES = (("xyz", 0, 16), ("yzx", 16, 32), ("yzx", 32, 64), ("xzy", 64, 80), ("xzy", 80, 112))
 ROUTE_ORDER = (3, 1, 4, 2, 0)
 NR = len(ROUTES)
-GROUPS = ((1, 3), (0, 2, 4))
+GROUPS = ((1, 3), (2,), (0, 4))
 HAND_TIME = 2.5
 HALF_K = WIDTH // 2
 STRIPS = ((0, 0, 2), (1, 0, 2), (2, 0, 1), (2, 1, 1), (3, 0, 2), (4, 0, 1), (4, 1, 1))
@@ -42,8 +42,8 @@
 
 
 def plan():
-    rate, latency = 46.6e3, 2.2
-    busy, queue, events, ids = {}, [], [], {}
+    rate, latency = 43.5e3, 2.2
+    busy, queue, ids = {}, [], {}
     serial = 0
 
     def push(at, event):
@@ -60,64 +60,74 @@
         outs.append((item, axis, sign))
         push(busy[axis, sign] + latency, ("item", route, item, sign))
 
-    at = 10.0
+    at = 12.4
     for route in ROUTE_ORDER:
         at += (ROUTES[route][2] - ROUTES[route][1]) / ROWS * 9.8
         push(at, ("own", route, None, 0))
-    left = {}
-    ready = {}
-    while queue:
-        at, _, (kind, route, item, sign) = heapq.heappop(queue)
-        one, two, three = ROUTES[route][0]
-        outs = []
-        if kind == "own":
-            left[route] = RINGS[one] - 1
-            for s in (1, -1):
-                if reach(RINGS[one], s, route):
-                    send(at, route, (1, s, 0), one, s, outs)
-        elif item[0] == 1:
-            if abs(item[1]) < reach(RINGS[one], sign, route):
-                send(at, route, (1, item[1] + sign, 0), one, sign, outs)
-            left[route] -= 1
-            if left[route] == 0:
-                for s in (1, -1):
-                    send(at, route, (2, s, 0), two, s, outs)
-                for s in (1, -1):
-                    send(at, route, (3, 0, s), three, s, outs)
-        elif item[0] == 2:
-            if abs(item[1]) < reach(RINGS[two], sign, route + 1):
-                send(at, route, (2, item[1] + sign, 0), two, sign, outs)
-            for s in (1, -1):
-                send(at, route, (3, item[1], s), three, s, outs)
-        else:
-            if abs(item[2]) < reach(RINGS[three], sign, item[1]):
-                send(at, route, (3, item[1], item[2] + sign), three, sign, outs)
-        z = distance(route, item or (1, 0, 0))
-        ready[route, z] = at
-        events.append((at, (kind, route, item, outs)))
-
+    left, steps, when = {}, [], {}
+    missing = {(route, z): 16 for route in range(NR) for z in range(8)}
     fill = [("strip", n, 1.2) for n in range(len(STRIPS))]
     fill += [("table", n, 0.8) for n in range(len(TABLE_ROWS))]
-    units = sorted((max(ready[route, z] for route in group), group, z) for group in GROUPS for z in range(8))
-    ends = {}
-    for far, need in ((0, (0, 1, 7)), (1, (1, 2, 3)), (3, (5, 6, 7)), (2, (3, 4, 5))):
-        ends.setdefault(max(n for n, u in enumerate(units) if u[2] in need), []).append(far)
-    work = []
-    for n, (when, group, z) in enumerate(units):
-        work.append((("unit", group, z), 0.5 * len(group), when))
-        work += [(("finish", far), 0.8, when) for far in ends.get(n, ())]
-    steps = []
-    clock = 8.5
-    for at, event in events:
-        while fill and at - clock >= 0.6 * fill[0][2]:
+    units = [(group, z) for group in GROUPS for z in range(8)]
+    ends = [(0, (0, 1, 7)), (1, (1, 2, 3)), (3, (5, 6, 7)), (2, (3, 4, 5))]
+    clock = 9.0
+    while queue or units or ends:
+        if queue and queue[0][0] <= clock:
+            at, _, (kind, route, item, sign) = heapq.heappop(queue)
+            clock += 0.12
+            one, two, three = ROUTES[route][0]
+            outs = []
+            if kind == "own":
+                clock += 0.2
+                left[route] = RINGS[one] - 1
+                for s in (1, -1):
+                    if reach(RINGS[one], s, route):
+                        send(clock, route, (1, s, 0), one, s, outs)
+            elif item[0] == 1:
+                if abs(item[1]) < reach(RINGS[one], sign, route):
+                    send(clock, route, (1, item[1] + sign, 0), one, sign, outs)
+                left[route] -= 1
+                if left[route] == 0:
+                    for s in (1, -1):
+                        send(clock, route, (2, s, 0), two, s, outs)
+                    for s in (1, -1):
+                        send(clock, route, (3, 0, s), three, s, outs)
+            elif item[0] == 2:
+                if abs(item[1]) < reach(RINGS[two], sign, route + 1):
+                    send(clock, route, (2, item[1] + sign, 0), two, sign, outs)
+                for s in (1, -1):
+                    send(clock, route, (3, item[1], s), three, s, outs)
+            else:
+                if abs(item[2]) < reach(RINGS[three], sign, item[1]):
+                    send(clock, route, (3, item[1], item[2] + sign), three, sign, outs)
+            z = distance(route, item or (1, 0, 0))
+            missing[route, z] -= 1 if kind == "own" or item[0] == 1 else RINGS[one]
+            when[route, z] = clock + HAND_TIME
+            steps.append((kind, route, item, outs))
+            continue
+        soon = queue[0][0] if queue else 1e9
+        if fill and (soon - clock >= 0.6 * fill[0][2]):
             steps.append(fill[0][:2])
             clock += fill.pop(0)[2]
-        while work and not fill and work[0][2] < at and work[0][2] + HAND_TIME <= max(clock, at):
-            steps.append(work[0][0])
-            clock = max(clock, work[0][2] + HAND_TIME) + work.pop(0)[1]
-        clock = max(clock, at) + 0.12
-        steps.append(event)
-    steps += [entry[:2] for entry in fill] + [entry[0] for entry in work]
+            continue
+        able = [
+            (max(when[route, z] for route in group), group, z)
+            for group, z in units
+            if not fill and not any(missing[route, z] for route in group)
+        ]
+        able.sort()
+        if able and able[0][0] <= clock:
+            _, group, z = able[0]
+            tall = sum(ROUTES[route][2] - ROUTES[route][1] for route in group)
+            steps.append(("unit", group, z))
+            units.remove((group, z))
+            clock += 2 * (0.1 + 0.143 * tall / 16)
+            for end in [e for e in ends if not any(z in e[1] for _, z in units)]:
+                steps.append(("finish", end[0]))
+                ends.remove(end)
+                clock += 0.5
+            continue
+        clock = min([soon] + [entry[0] for entry in able])
     return steps, ids
 
 
@@ -160,7 +170,7 @@
 
     loads = [
         load(fast_gain_in, fast_gain, 0),
-        load(slow_gain_in, slow_gain.at[0:1], 1),
+        load(slow_gain_in, slow_gain, 1),
         load(slow_in, slow, 2),
         load(pos_in, pos, 3),
         load(tok_in, tok, 4),
@@ -183,8 +193,8 @@
     lax.fori_loop(0, 8, clear, 0)
     for copy in loads[:2]:
         copy.wait()
-    lanes = lax.broadcasted_iota(jnp.int32, (8, 128), 1)
-    gain[...] = jnp.where(lanes < 14, slow_gain[...], 0.0)
+    gain[...] = jnp.zeros((8, 128), jnp.float32)
+    gain[0:1, 0:14] = slow_gain[...]
     gain[...] = pltpu.roll(gain[...], r * 14, 1)
     gain[1:2, :] = gain[0:1, :]
     gain[0:1, :] = jnp.zeros((1, 128), jnp.float32)
@@ -462,7 +472,7 @@
             vmem((3, ROWS, COLS), bf16),
             vmem((ROWS, COLS), f32),
             vmem((1, ROWS), bf16),
-            vmem((8, 128), f32),
+            vmem((1, 14), f32),
             vmem((1, TOK), jnp.int32),
             vmem((8, 128), f32),
             vmem((8, 128), f32),
@@ -487,7 +497,7 @@
         ),
     )(
         tokens, fast_weight[0], slow_weight, fast_gain,
-        jnp.pad(slow_gain.reshape(1, 14), ((0, 0), (0, 114))), positions.reshape(1, TOK),
+        slow_gain.reshape(1, 14), positions.reshape(1, TOK),
     )
     q, k, v, new_weight, new_gain = pl.pallas_call(
         flush,

time: 101 us -> 93.1 us (0.922)
  Pallas kernels: 99.2 us -> 92.2 us
  local copies, waits for them, and re-layouts: 1.17 us -> 0 us
    pallas_call x1, Pallas kernels: 97.1 us -> 90.2 us  [on_device(): pl.pallas_call(functools.partial(kernel, steps, ids), out_shape=tuple((vm...]
    pad x1 -> x0, local copies, waits for them, and re-layouts: 1.17 us -> none  [on_device(): jnp.pad(slow_gain.reshape(1, 14), ((0, 0), (0, 114)))]
where the time goes in v3:
time: 93.1 us; the launch traced here: 93 us
  Pallas kernels  92.2 us (99%)
    pallas_call x1, Pallas kernels, on_device(): pl.pallas_call(functools.partial(kernel, steps, ids), out_shape=tuple((vm...  90.2 us
    pallas_call x1, Pallas kernels, on_device(): pl.pallas_call(flush, out_shape=tuple((jax.ShapeDtypeStruct(*s) for s in...  2.03 us

profile of v3, /device:TPU:1, one launch (start us, length us, event | category | flops | bytes accessed | tf_op | source)
XLA Modules:
  0.0 93.0 jit_solution(12477517650638875957)
XLA Ops:
  0.6 90.2 %shard_map.101 = (bf16[480,2048]{1,0:T(8,128)(2,1)S(1)}, bf16[480,1024]{1,0:T(8,128)(2,1)S(1)}, bf16[480,1024]{1,0:T(8,128)(2,1)S(1)}, f32[112,512]{1,0:T(8,128)S(1)}, f32[1,14]{1,0:T(1,128)S(1)}) custom-call(bf16[480,3584]{1,0:T(8,128)(2,1)} %tok_in.1, bf16[112,4096]{1,0:T(8,128)(2,1)} %bitcast.4, f32[112,512]{1,0:T(8,128)} %slow_in.1, ...), custom_call_target="tpu_custom_call" | custom-call | tf_op jit(solution)/shard_map/pallas_call | solution.py:458
  90.8 2.0 %shard_map.102 = (bf16[480,2048]{1,0:T(8,128)(2,1)}, bf16[480,1024]{1,0:T(8,128)(2,1)}, bf16[480,1024]{1,0:T(8,128)(2,1)}, f32[112,512]{1,0:T(8,128)}, f32[1,14]{1,0:T(1,128)}) custom-call(bf16[480,2048]{1,0:T(8,128)(2,1)S(1)} %get-tuple-element.15.refs_0_, bf16[480,1024]{1,0:T(8,128)(2,1)S(1)} %get-tuple-element.16.refs_1_, ...), custom_call_target="tpu_custom_call" | custom-call | tf_op jit(solution)/shard_map/pallas_call | solution.py:502

commit v4 on v3

--- a/solution.py
+++ b/solution.py
@@ -23,8 +23,8 @@
 ROUTES = (("xyz", 0, 16), ("yzx", 16, 32), ("yzx", 32, 64), ("xzy", 64, 80), ("xzy", 80, 112))
 ROUTE_ORDER = (3, 1, 4, 2, 0)
 NR = len(ROUTES)
-GROUPS = ((1, 3), (2,), (0, 4))
-HAND_TIME = 2.5
+GROUPS = ((1, 3), (0, 2, 4))
+HAND_TIME = 2.0
 HALF_K = WIDTH // 2
 STRIPS = ((0, 0, 2), (1, 0, 2), (2, 0, 1), (2, 1, 1), (3, 0, 2), (4, 0, 1), (4, 1, 1))
 TABLE_ROWS = ((0, 128), (128, 128), (256, 128), (384, 96))
@@ -68,8 +68,9 @@
     missing = {(route, z): 16 for route in range(NR) for z in range(8)}
     fill = [("strip", n, 1.2) for n in range(len(STRIPS))]
     fill += [("table", n, 0.8) for n in range(len(TABLE_ROWS))]
-    units = [(group, z) for group in GROUPS for z in range(8)]
-    ends = [(0, (0, 1, 7)), (1, (1, 2, 3)), (3, (5, 6, 7)), (2, (3, 4, 5))]
+    units = [(group, z, side) for group in GROUPS for z in range(8) for side in (0, 1)]
+    need = ((0, (0, 1, 7)), (1, (1, 2, 3)), (3, (5, 6, 7)), (2, (3, 4, 5)))
+    ends = [(far, zs, side) for far, zs in need for side in (0, 1)]
     clock = 9.0
     while queue or units or ends:
         if queue and queue[0][0] <= clock:
@@ -102,7 +103,7 @@
                     send(clock, route, (3, item[1], item[2] + sign), three, sign, outs)
             z = distance(route, item or (1, 0, 0))
             missing[route, z] -= 1 if kind == "own" or item[0] == 1 else RINGS[one]
-            when[route, z] = clock + HAND_TIME
+            when[route, z] = clock
             steps.append((kind, route, item, outs))
             continue
         soon = queue[0][0] if queue else 1e9
@@ -111,21 +112,21 @@
             clock += fill.pop(0)[2]
             continue
         able = [
-            (max(when[route, z] for route in group), group, z)
-            for group, z in units
+            (max(when[route, z] for route in group) + HAND_TIME * side, group, z, side)
+            for group, z, side in units
             if not fill and not any(missing[route, z] for route in group)
         ]
         able.sort()
         if able and able[0][0] <= clock:
-            _, group, z = able[0]
+            _, group, z, side = able[0]
             tall = sum(ROUTES[route][2] - ROUTES[route][1] for route in group)
-            steps.append(("unit", group, z))
-            units.remove((group, z))
-            clock += 2 * (0.1 + 0.143 * tall / 16)
-            for end in [e for e in ends if not any(z in e[1] for _, z in units)]:
-                steps.append(("finish", end[0]))
+            steps.append(("unit", group, z, side))
+            units.remove((group, z, side))
+            clock += 0.1 + 0.143 * tall / 16
+            for end in [e for e in ends if not any(u[1] in e[1] and u[2] == e[2] for u in units)]:
+                steps.append(("finish", end[0], end[2]))
                 ends.remove(end)
-                clock += 0.5
+                clock += 0.25
             continue
         clock = min([soon] + [entry[0] for entry in able])
     return steps, ids
@@ -340,57 +341,43 @@
             else:
                 strips[parity, :, to : to + 256] = moved
 
-    def unit(group, far):
-        for route in group:
-            some = bufs[route].at[1 - c, pl.ds(0, 16)]
-            remote(some, some, hand_send.at[route], hand_recv.at[route * 8 + far], partner).wait_recv()
+    def unit(group, far, side):
+        if side:
+            for route in group:
+                some = bufs[route].at[1 - c, pl.ds(0, 16)]
+                remote(some, some, hand_send.at[route], hand_recv.at[route * 8 + far], partner).wait_recv()
         wz = wrap(z, -far, 8)
-
-        def of_core(bc, _):
-            parts = [
-                bufs[route][bc, spot(route, px, py, wz)] for route in group for py in range(4) for px in range(4)
-            ]
-            lanes = [
-                strips[lax.rem(wz, 2), :, 16 * ROUTES[route][1] : 16 * ROUTES[route][2]] for route in group
-            ]
-            acc[(wz // 2) * 2 + bc] += jnp.dot(
-                jnp.concatenate(lanes, axis=1), jnp.concatenate(parts, axis=0), preferred_element_type=jnp.float32
-            )
-            return 0
-
-        lax.fori_loop(0, 2, of_core, 0)
-
-    def finish(far):
-        bz = wrap(zh, -far, 4)
-
-        def of_core(bc, _):
-            b = bz * 2 + bc
-
-            def turned(ref, first):
-                start = (b - first) * COLS
-                for h in range(0, COLS, HEAD):
-                    u, w = acc[b, :, h : h + 128], acc[b, :, h + 128 : h + 256]
-                    tc, ts = turn_c[0], turn_s[...]
-                    ref[:, pl.ds(pl.multiple_of(start + h, 128), 128)] = (u * tc - w * ts).astype(jnp.bfloat16)
-                    ref[:, pl.ds(pl.multiple_of(start + h + 128, 128), 128)] = (w * tc + u * ts).astype(jnp.bfloat16)
-
-            @pl.when(b < 4)
-            def _():
-                turned(q_out, 0)
-
-            @pl.when((b >= 4) & (b < 6))
-            def _():
-                turned(k_out, 4)
-
-            @pl.when(b >= 6)
-            def _():
-                for h in range(0, COLS, 128):
-                    cols = pl.ds(pl.multiple_of((b - 6) * COLS + h, 128), 128)
-                    v_out[:, cols] = (acc[b, :, h : h + 128] * turn_c[1]).astype(jnp.bfloat16)
-
-            return 0
-
-        lax.fori_loop(0, 2, of_core, 0)
+        bc = 1 - c if side else c
+        parts = [bufs[route][bc, spot(route, px, py, wz)] for route in group for py in range(4) for px in range(4)]
+        lanes = [strips[lax.rem(wz, 2), :, 16 * ROUTES[route][1] : 16 * ROUTES[route][2]] for route in group]
+        acc[(wz // 2) * 2 + bc] += jnp.dot(
+            jnp.concatenate(lanes, axis=1), jnp.concatenate(parts, axis=0), preferred_element_type=jnp.float32
+        )
+
+    def finish(far, side):
+        b = wrap(zh, -far, 4) * 2 + (1 - c if side else c)
+
+        def turned(ref, first):
+            start = (b - first) * COLS
+            for h in range(0, COLS, HEAD):
+                u, w = acc[b, :, h : h + 128], acc[b, :, h + 128 : h + 256]
+                tc, ts = turn_c[0], turn_s[...]
+                ref[:, pl.ds(pl.multiple_of(start + h, 128), 128)] = (u * tc - w * ts).astype(jnp.bfloat16)
+                ref[:, pl.ds(pl.multiple_of(start + h + 128, 128), 128)] = (w * tc + u * ts).astype(jnp.bfloat16)
+
+        @pl.when(b < 4)
+        def _():
+            turned(q_out, 0)
+
+        @pl.when((b >= 4) & (b < 6))
+        def _():
+            turned(k_out, 4)
+
+        @pl.when(b >= 6)
+        def _():
+            for h in range(0, COLS, 128):
+                cols = pl.ds(pl.multiple_of((b - 6) * COLS + h, 128), 128)
+                v_out[:, cols] = (acc[b, :, h : h + 128] * turn_c[1]).astype(jnp.bfloat16)
 
     first_strip, first_table, first_own = True, True, True
     for step in steps:
@@ -407,7 +394,7 @@
         elif step[0] == "unit":
             unit(*step[1:])
         elif step[0] == "finish":
-            finish(step[1])
+            finish(*step[1:])
         else:
             kind, route, item, outs = step
             if kind == "own":

time: 93.1 us -> 92.3 us (level)
  no operation moved by 1% of the time
where the time goes in v4:
time: 92.3 us; the launch traced here: 92.2 us
  Pallas kernels  91.4 us (99%)
    pallas_call x1, Pallas kernels, on_device(): pl.pallas_call(functools.partial(kernel, steps, ids), out_shape=tuple((vm...  89.4 us
    pallas_call x1, Pallas kernels, on_device(): pl.pallas_call(flush, out_shape=tuple((jax.ShapeDtypeStruct(*s) for s in...  2.03 us

profile of v4, /device:TPU:1, one launch (start us, length us, event | category | flops | bytes accessed | tf_op | source)
XLA Modules:
  0.0 92.2 jit_solution(8987360765208915748)
XLA Ops:
  0.6 89.4 %shard_map.101 = (bf16[480,2048]{1,0:T(8,128)(2,1)S(1)}, bf16[480,1024]{1,0:T(8,128)(2,1)S(1)}, bf16[480,1024]{1,0:T(8,128)(2,1)S(1)}, f32[112,512]{1,0:T(8,128)S(1)}, f32[1,14]{1,0:T(1,128)S(1)}) custom-call(bf16[480,3584]{1,0:T(8,128)(2,1)} %tok_in.1, bf16[112,4096]{1,0:T(8,128)(2,1)} %bitcast.4, f32[112,512]{1,0:T(8,128)} %slow_in.1, ...), custom_call_target="tpu_custom_call" | custom-call | tf_op jit(solution)/shard_map/pallas_call | solution.py:445
  90.0 2.0 %shard_map.102 = (bf16[480,2048]{1,0:T(8,128)(2,1)}, bf16[480,1024]{1,0:T(8,128)(2,1)}, bf16[480,1024]{1,0:T(8,128)(2,1)}, f32[112,512]{1,0:T(8,128)}, f32[1,14]{1,0:T(1,128)}) custom-call(bf16[480,2048]{1,0:T(8,128)(2,1)S(1)} %get-tuple-element.15.refs_0_, bf16[480,1024]{1,0:T(8,128)(2,1)S(1)} %get-tuple-element.16.refs_1_, ...), custom_call_target="tpu_custom_call" | custom-call | tf_op jit(solution)/shard_map/pallas_call | solution.py:489
